TPU v7x, 32 devices: a whole 2x2x4 slice. The times are simulated.
32 devices in a mesh: row: 4 (over z), col: 4 (over x, core), depth: 2 (over y).
Axes of the slice: x: 2, y: 2, z: 4, core: 2. Of those that a mesh axis runs over, the one named last changes fastest.
Arguments:
- tokens: bfloat16 [2048, 8192], P(('row', 'col'), 'depth'), may hold values from -0.3125 to 0.3125
- weight: bfloat16 [8192, 8192], P('depth', ('col', 'row')), may hold values from -0.0625 to 0.0625
- grad_output: bfloat16 [2048, 8192], P('row', ('col', 'depth')), may hold values from -6 to 6
Outputs:
- grad_input: bfloat16 [2048, 8192], P(('row', 'col'), 'depth')
- grad_weight: bfloat16 [8192, 8192], P('depth', ('col', 'row'))
All inputs are finite; a program needn't handle non-finite values.
Results may differ from a plain program's by a relative error of at most 0.001.
Values may be sent and summed in bfloat16 or wider, within the bound.
A program may use at most 128 MiB of HBM per device.

v0:
```python
import jax
import jax.numpy as jnp
from jax import lax
from jax.sharding import PartitionSpec as P

last_with_last = (((1,), (1,)), ((), ()))
first_with_first = (((0,), (0,)), ((), ()))


def input_grads(weight, grad_block):
    weight_block = lax.all_gather(weight, "row", axis=1, tiled=True)
    partial_value = lax.dot_general(
        grad_block, weight_block, last_with_last, preferred_element_type=jnp.float32
    )
    column_slab = lax.psum_scatter(partial_value, "col", scatter_dimension=1, tiled=True).astype(
        jnp.bfloat16
    )
    return lax.all_to_all(column_slab, "col", split_axis=0, concat_axis=1, tiled=True)


def weight_grads(tokens, grad_block):
    partial_value = lax.dot_general(
        lax.all_gather(tokens, "col", axis=0, tiled=True),
        grad_block,
        first_with_first,
        preferred_element_type=jnp.float32,
    )
    return lax.psum_scatter(partial_value, "row", scatter_dimension=1, tiled=True).astype(
        jnp.bfloat16
    )


def per_device(tokens, weight, grad_output):
    grad_block = lax.all_gather(grad_output, "depth", axis=1, tiled=True)
    grad_input = input_grads(weight, grad_block)
    grad_weight = weight_grads(tokens, grad_block)
    return (grad_input, grad_weight)


def solution(mesh):
    return jax.shard_map(
        per_device,
        mesh=mesh,
        in_specs=(
            P(("row", "col"), "depth"),
            P("depth", ("col", "row")),
            P("row", ("col", "depth")),
        ),
        out_specs=(P(("row", "col"), "depth"), P("depth", ("col", "row"))),
        check_vma=False,
    )
```

profile of v0, /device:TPU:0, one launch (start us, length us, event | category | flops | bytes accessed | tf_op | source)
XLA Modules:
  0.0 1008.6 jit_solution(7018529357525210481)
XLA Ops:
  7.2 0.0 all-gather.4.cloned.1.call-start
  7.2 0.7 all-gather.4.cloned.1.call-update
  7.9 0.0 all-gather.6.cloned.1.call-start
  7.9 0.7 all-gather.6.cloned.1.call-update
  8.6 0.0 all-gather.8.cloned.1.call-start
  8.7 0.7 all-gather.8.cloned.1.call-update
  9.4 0.0 reduce-scatter.3.cloned.1.call-start
  9.4 35.9 %all-gather.4.cloned.1.call-done = bf16[512,2048]{1,0:T(8,128)(2,1)} async-done(((bf16[512,1024]{1,0:T(8,128)(2,1)}), bf16[512,2048]{1,0:T(8,128)(2,1)}) %all-gather.4.cloned.1.call-update) | async-done | bytes 2097168 | tf_op jit(solution)/shard_map/all_gather | solution.py:34
  45.4 288.4 %all-gather.6.cloned.1.call-done = bf16[4096,2048]{1,0:T(8,128)(2,1)} async-done(((bf16[4096,512]{1,0:T(8,128)(2,1)}), bf16[4096,2048]{1,0:T(8,128)(2,1)}) %all-gather.6.cloned.1.call-update) | async-done | bytes 16777232 | tf_op jit(solution)/shard_map/all_gather | solution.py:11
  333.7 15.1 %fusion = f32[512,4096]{1,0:T(8,128)} fusion(bf16[512,2048]{1,0:T(8,128)(2,1)} %all-gather.4.cloned.1.call-done, bf16[4096,2048]{1,0:T(8,128)(2,1)} %all-gather.6.cloned.1.call-done), kind=kOutput, calls=%fused_computation | convolution fusion | flops 8589934592 | bytes 27262976 | tf_op jit(solution)/shard_map/dot_general | solution.py:12
  348.8 0.0 copy-start
  348.8 0.0 reduce-scatter.3.cloned.1.call-update
  348.8 0.0 reduce-scatter.5.cloned.1.call-start
  348.9 19.1 %all-gather.8.cloned.1.call-done = bf16[512,4096]{1,0:T(8,128)(2,1)} async-done(((bf16[128,4096]{1,0:T(8,128)(2,1)}), bf16[512,4096]{1,0:T(8,128)(2,1)}) %all-gather.8.cloned.1.call-update) | async-done | bytes 4194320 | tf_op jit(solution)/shard_map/all_gather | solution.py:23
  368.0 0.0 copy-done
  368.0 21.6 %fusion.1 = f32[4096,2048]{1,0:T(8,128)} fusion(bf16[512,4096]{1,0:T(8,128)(2,1)} %all-gather.8.cloned.1.call-done, bf16[512,2048]{1,0:T(8,128)(2,1)S(1)} %copy-done), kind=kOutput, calls=%fused_computation.1 | convolution fusion | flops 8589934592 | bytes 39845888 | tf_op jit(solution)/shard_map/dot_general | solution.py:22
  389.5 0.0 reduce-scatter.5.cloned.1.call-update
  389.6 52.2 %reduce-scatter.3.cloned.1.call-done = f32[512,1024]{1,0:T(8,128)} async-done(((f32[512,4096]{1,0:T(8,128)}), f32[512,1024]{1,0:T(8,128)}) %reduce-scatter.3.cloned.1.call-update) | async-done | bytes 2097168 | tf_op jit(solution)/shard_map/reduce_scatter | solution.py:15
  441.7 1.7 convert_element_type.6
  443.5 16.9 %all_to_all.19 = bf16[4,128,1024]{2,1,0:T(8,128)(2,1)S(1)} all-to-all(bf16[4,128,1024]{2,1,0:T(8,128)(2,1)S(1)} %bitcast.8), channel_id=1, replica_groups=mesh['row'=4,'col'=4,'depth'=2] {'col'}, dimensions={0} | all-to-all | bytes 2097152 | tf_op jit(solution)/shard_map/all_to_all | solution.py:18
  460.3 1.1 copy.6
  461.4 534.8 %reduce-scatter.5.cloned.1.call-done = f32[4096,512]{1,0:T(8,128)} async-done(((f32[4096,2048]{1,0:T(8,128)}), f32[4096,512]{1,0:T(8,128)}) %reduce-scatter.5.cloned.1.call-update) | async-done | bytes 8388624 | tf_op jit(solution)/shard_map/reduce_scatter | solution.py:28
  996.1 5.9 convert_element_type.7
Async XLA Ops:
  7.2 38.2 %all-gather.4.cloned.1.call-start = ((), (), s32[]{:S(2)}) async-start(), calls=%async_computation.3 | async-start | bytes 3145728 | tf_op jit(solution)/shard_map/all_gather | solution.py:34
  7.9 325.8 %all-gather.6.cloned.1.call-start = ((), (), s32[]{:S(2)}) async-start(), calls=%async_computation.4 | async-start | bytes 20971520 | tf_op jit(solution)/shard_map/all_gather | solution.py:11
  8.6 359.3 %all-gather.8.cloned.1.call-start = ((), (), s32[]{:S(2)}) async-start(), calls=%async_computation.6 | async-start | bytes 5242880 | tf_op jit(solution)/shard_map/all_gather | solution.py:23
  9.4 432.3 %reduce-scatter.3.cloned.1.call-start = ((), (), s32[]{:S(2)}) async-start(), calls=%async_computation.5 | async-start | bytes 10485760 | tf_op jit(solution)/shard_map/reduce_scatter | solution.py:15
  348.8 19.2 %copy-start = (bf16[512,2048]{1,0:T(8,128)(2,1)S(1)}, bf16[512,2048]{1,0:T(8,128)(2,1)}, u32[]{:S(2)}) copy-start(bf16[512,2048]{1,0:T(8,128)(2,1)} %all-gather.4.cloned.1.call-done) | copy-start | bytes 6291460
  348.8 647.3 %reduce-scatter.5.cloned.1.call-start = ((), (), s32[]{:S(2)}) async-start(), calls=%async_computation.7 | async-start | bytes 41943040 | tf_op jit(solution)/shard_map/reduce_scatter | solution.py:28
Sparse Core Ops, SparseCore 0:
  9.5 35.8 all-gather.3
  46.9 286.7 all-gather.5
  335.3 32.6 all-gather.7
  370.4 71.2 reduce-scatter.2
  443.9 552.1 reduce-scatter.4
where the time goes:
time: 1010 us
  waiting for transfers between devices  932 us (92%)
  matrix products  36.6 us (4%)
  blocking collectives  16.9 us (2%)
  between operations  13.8 us (1%)
    reduce_scatter x1, waiting for transfers between devices, weight_grads(): lax.psum_scatter(partial_value, 'row', scatter_dimension=1, tiled=True)  535 us
    all_gather x1, waiting for transfers between devices, input_grads(): weight_block = lax.all_gather(weight, 'row', axis=1, tiled=True)  288 us
    reduce_scatter x1, waiting for transfers between devices, input_grads(): lax.psum_scatter(partial_value, 'col', scatter_dimension=1, tiled=True)  52.2 us
    all_gather x1, waiting for transfers between devices, per_device(): grad_block = lax.all_gather(grad_output, 'depth', axis=1, tiled=True)  35.9 us
    dot_general x1, matrix products, weight_grads(): lax.dot_general(lax.all_gather(tokens, 'col', axis=0, tiled=True), grad_b...  21.6 us
  transfers between devices with their start and end apart: 5, of which 5 were waited for; matrix products, arithmetic and copies ran while one was open for 4% of the time, Pallas kernels for 0%

commit v1 on v0

--- a/solution.py
+++ b/solution.py
@@ -8,7 +8,20 @@
 
 
 def input_grads(weight, grad_block):
-    weight_block = lax.all_gather(weight, "row", axis=1, tiled=True)
+
+    def deliver_patches(local_x):
+        nd = jax.lax.axis_size("row")
+        row_list = tuple(((k, (k + 1) % nd) for k in range(nd)))
+        x_now = [None] * nd
+        x_now[nd - 1] = local_x
+        for no in range(nd - 2, -1, -1):
+            x_now[no] = jax.lax.ppermute(x_now[no + 1], axis_name="row", perm=row_list)
+        spare = jnp.concatenate(x_now, 1)
+        even = jax.lax.axis_index("row")
+        small = (even + 1) * local_x.shape[1]
+        return jnp.roll(spare, small, 1)
+
+    weight_block = deliver_patches(weight)
     partial_value = lax.dot_general(
         grad_block, weight_block, last_with_last, preferred_element_type=jnp.float32
     )

time: 1010 us -> 973 us (0.963)
  waiting for transfers between devices: 932 us -> 863 us
  local copies, waits for them, and re-layouts: 1.07 us -> 30.5 us
    all_gather x1 -> x0, waiting for transfers between devices: 288 us -> none  [input_grads(): weight_block = lax.all_gather(weight, 'row', axis=1, tiled=True)]
    ppermute x0 -> x3, waiting for transfers between devices: none -> 279 us  [deliver_patches(): x_now[no] = jax.lax.ppermute(x_now[no + 1], axis_name='row', perm=row_list)]
    all_gather x1, waiting for transfers between devices: 35.9 us -> 0.01 us  [per_device(): grad_block = lax.all_gather(grad_output, 'depth', axis=1, tiled=True)]
    unnamed x2 -> x16, local copies, waits for them, and re-layouts: 0.01 us -> 28.2 us
    all_gather x1, waiting for transfers between devices: 19.1 us -> 0.02 us  [weight_grads(): lax.all_gather(tokens, 'col', axis=0, tiled=True)]
  transfers between devices with their start and end apart: 5 -> 7, of which waited for: 5 -> 5; matrix products, arithmetic and copies ran while one was open for 4% -> 7% of each run, Pallas kernels for 0% -> 0%
where the time goes in v1:
time: 973 us
  waiting for transfers between devices  863 us (89%)
  matrix products  37.3 us (4%)
  local copies, waits for them, and re-layouts  30.5 us (3%)
  blocking collectives  16.9 us (2%)
  between operations  13.8 us (1%)
    reduce_scatter x1, waiting for transfers between devices, weight_grads(): lax.psum_scatter(partial_value, 'row', scatter_dimension=1, tiled=True)  535 us
    ppermute x3, waiting for transfers between devices, deliver_patches(): x_now[no] = jax.lax.ppermute(x_now[no + 1], axis_name='row', perm=row_list)  279 us
    reduce_scatter x1, waiting for transfers between devices, input_grads(): lax.psum_scatter(partial_value, 'col', scatter_dimension=1, tiled=True)  49 us
    unnamed x16, local copies, waits for them, and re-layouts  28.2 us
    dot_general x1, matrix products, weight_grads(): lax.dot_general(lax.all_gather(tokens, 'col', axis=0, tiled=True), grad_b...  20 us
  transfers between devices with their start and end apart: 7, of which 5 were waited for; matrix products, arithmetic and copies ran while one was open for 7% of the time, Pallas kernels for 0%

profile of v1, /device:TPU:0, one launch (start us, length us, event | category | flops | bytes accessed | tf_op | source)
XLA Modules:
  0.0 972.6 jit_solution(14187249734127800834)
XLA Ops:
  7.2 3.1 collective-permute-start
  10.3 92.8 %collective-permute-done = bf16[4096,512]{1,0:T(8,128)(2,1)S(1)} collective-permute-done((bf16[4096,512]{1,0:T(8,128)(2,1)}, bf16[4096,512]{1,0:T(8,128)(2,1)S(1)}, u32[]{:S(2)}, u32[]{:S(2)}) %collective-permute-start) | collective-permute-done | bytes 4194336 | tf_op jit(solution)/shard_map/ppermute | solution.py:18
  103.1 2.0 copy-done.1
  105.1 93.6 %collective-permute-done.1 = bf16[4096,512]{1,0:T(8,128)(2,1)} collective-permute-done((bf16[4096,512]{1,0:T(8,128)(2,1)S(1)}, bf16[4096,512]{1,0:T(8,128)(2,1)}, u32[]{:S(2)}, u32[]{:S(2)}) %collective-permute-start.1) | collective-permute-done | bytes 4194336 | tf_op jit(solution)/shard_map/ppermute | solution.py:18
  198.8 0.0 all-gather.5.cloned.1.call-start
  198.9 0.7 all-gather.5.cloned.1.call-update
  199.6 92.1 %collective-permute-done.2 = bf16[4096,512]{1,0:T(8,128)(2,1)} collective-permute-done((bf16[4096,512]{1,0:T(8,128)(2,1)}, bf16[4096,512]{1,0:T(8,128)(2,1)}, u32[]{:S(2)}, u32[]{:S(2)}) %collective-permute-start.2) | collective-permute-done | bytes 4194336 | tf_op jit(solution)/shard_map/ppermute | solution.py:18
  291.8 4.5 constant_dynamic-update-slice_fusion.7
  296.2 4.5 constant_dynamic-update-slice_fusion.6
  300.7 2.3 constant_dynamic-update-slice_fusion.5
  303.0 2.3 constant_dynamic-update-slice_fusion.4
  305.4 4.5 constant_dynamic-update-slice_fusion.3
  309.8 4.5 constant_dynamic-update-slice_fusion.2
  314.3 2.3 constant_dynamic-update-slice_fusion.1
  316.7 2.3 constant_dynamic-update-slice_fusion
  318.9 17.3 %fusion.2 = f32[512,4096]{0,1:T(8,128)} fusion(bf16[512,2048]{1,0:T(8,128)(2,1)} %all-gather.3.cloned.1.call-done, bf16[4096,4096]{1,0:T(8,128)(2,1)} %constant_dynamic-update-slice_fusion, s32[]{:T(128)S(6)} %select_n.14), kind=kOutput, calls=%fused_computation.2 | convolution fusion | flops 8589934592 | bytes 27262980 | tf_op jit(solution)/shard_map/dot_general | solution.py:25
  336.3 0.2 reduce-scatter.5.cloned.1.call-start
  336.6 20.0 %fusion.6 = f32[4096,2048]{1,0:T(8,128)} fusion(bf16[512,4096]{1,0:T(8,128)(2,1)} %all-gather.5.cloned.1.call-done, bf16[512,2048]{1,0:T(8,128)(2,1)S(1)} %copy-done.3), kind=kOutput, calls=%fused_computation.14 | convolution fusion | flops 8589934592 | bytes 39845888 | tf_op jit(solution)/shard_map/dot_general | solution.py:35
  356.6 49.0 %reduce-scatter.3.cloned.1.call-done = f32[512,1024]{0,1:T(8,128)} async-done(((f32[512,4096]{0,1:T(8,128)}), f32[512,1024]{0,1:T(8,128)}) %reduce-scatter.3.cloned.1.call-update) | async-done | bytes 2097168 | tf_op jit(solution)/shard_map/reduce_scatter | solution.py:28
  405.6 1.7 copy_bitcast_fusion
  407.4 16.9 %all_to_all.19 = bf16[4,128,1024]{1,2,0:T(8,128)(2,1)S(1)} all-to-all(bf16[4,128,1024]{1,2,0:T(8,128)(2,1)S(1)} %copy_bitcast_fusion), channel_id=1, replica_groups=mesh['row'=4,'col'=4,'depth'=2] {'col'}, dimensions={0} | all-to-all | bytes 2097152 | tf_op jit(solution)/shard_map/all_to_all | solution.py:31
  424.2 1.3 copy.7
  425.5 534.6 %reduce-scatter.5.cloned.1.call-done = f32[4096,512]{1,0:T(8,128)} async-done(((f32[4096,2048]{1,0:T(8,128)}), f32[4096,512]{1,0:T(8,128)}) %reduce-scatter.5.cloned.1.call-update) | async-done | bytes 8388624 | tf_op jit(solution)/shard_map/reduce_scatter | solution.py:41
  960.1 5.9 convert_element_type.7
  (16 shorter events, 0.2 us)
Async XLA Ops:
  7.2 311.8 %all-gather.3.cloned.1.call-start = ((), (), s32[]{:S(2)}) async-start(), calls=%async_computation.3 | async-start | bytes 3145728 | tf_op jit(solution)/shard_map/all_gather | solution.py:47
  7.2 95.9 %collective-permute-start = (bf16[4096,512]{1,0:T(8,128)(2,1)}, bf16[4096,512]{1,0:T(8,128)(2,1)S(1)}, u32[]{:S(2)}, u32[]{:S(2)}) collective-permute-start(bf16[4096,512]{1,0:T(8,128)(2,1)} %param.4), channel_id=1, source_target_pairs={{0,8},{8,16},{16,24},{24,0},{1,9},{9,17},{17,25},{25,1},{2,10},{10... | collective-permute-start | bytes 12582920 | tf_op jit(solution)/shard_map/ppermute | solution.py:18
  103.1 2.0 copy-start.1
  105.1 93.6 %collective-permute-start.1 = (bf16[4096,512]{1,0:T(8,128)(2,1)S(1)}, bf16[4096,512]{1,0:T(8,128)(2,1)}, u32[]{:S(2)}, u32[]{:S(2)}) collective-permute-start(bf16[4096,512]{1,0:T(8,128)(2,1)S(1)} %collective-permute-done), channel_id=1, source_target_pairs={{0,8},{8,16},{16,24},{24,0},{1,9},{9,17},{17,25},{25,1},{2,10},{10... | collective-permute-start | bytes 12582920 | tf_op jit(solution)/shard_map/ppermute | solution.py:18
  198.8 93.0 %collective-permute-start.2 = (bf16[4096,512]{1,0:T(8,128)(2,1)}, bf16[4096,512]{1,0:T(8,128)(2,1)}, u32[]{:S(2)}, u32[]{:S(2)}) collective-permute-start(bf16[4096,512]{1,0:T(8,128)(2,1)} %collective-permute-done.1), channel_id=1, source_target_pairs={{0,8},{8,16},{16,24},{24,0},{1,9},{9,17},{17,25},{25,1},{2,10},{10... | collective-permute-start | bytes 12582920 | tf_op jit(solution)/shard_map/ppermute | solution.py:18
  198.8 137.7 %all-gather.5.cloned.1.call-start = ((), (), s32[]{:S(2)}) async-start(), calls=%async_computation.5 | async-start | bytes 5242880 | tf_op jit(solution)/shard_map/all_gather | solution.py:36
  199.6 206.1 %reduce-scatter.3.cloned.1.call-start = ((), (), s32[]{:S(2)}) async-start(), calls=%async_computation.4 | async-start | bytes 10485760 | tf_op jit(solution)/shard_map/reduce_scatter | solution.py:28
  199.6 101.1 %copy-start.2 = (bf16[4096,512]{1,0:T(8,128)(2,1)S(1)}, bf16[4096,512]{1,0:T(8,128)(2,1)}, u32[]{:S(2)}) copy-start(bf16[4096,512]{1,0:T(8,128)(2,1)} %copy-done.1) | copy-start | bytes 12582916
  199.6 103.4 %copy-start = (bf16[4096,512]{1,0:T(8,128)(2,1)S(1)}, bf16[4096,512]{1,0:T(8,128)(2,1)}, u32[]{:S(2)}) copy-start(bf16[4096,512]{1,0:T(8,128)(2,1)} %param.4) | copy-start | bytes 12582916
  318.9 17.6 %copy-start.3 = (bf16[512,2048]{1,0:T(8,128)(2,1)S(1)}, bf16[512,2048]{1,0:T(8,128)(2,1)}, u32[]{:S(2)}) copy-start(bf16[512,2048]{1,0:T(8,128)(2,1)} %all-gather.3.cloned.1.call-done) | copy-start | bytes 6291460
  336.3 623.8 %reduce-scatter.5.cloned.1.call-start = ((), (), s32[]{:S(2)}) async-start(), calls=%async_computation.6 | async-start | bytes 41943040 | tf_op jit(solution)/shard_map/reduce_scatter | solution.py:41
Sparse Core Ops, SparseCore 0:
  198.9 34.3 all-gather.2
  234.9 34.4 all-gather.4
  336.4 69.1 reduce-scatter.2
  407.8 552.2 reduce-scatter.4
